TPU v7x, 256 devices: a whole 4x4x8 slice. The times are simulated.
256 devices in a mesh: row: 16 (over z_lo, y), col: 16 (over z_hi, x, core).
Axes of the slice: x: 4, y: 4, z: 8 (z_hi: 2, z_lo: 4; z = z_hi * 4 + z_lo), core: 2. Of those that a mesh axis runs over, the one named last changes fastest.
Arguments:
- orbitals: float32 [2048, 28672], P(('row', 'col')), may hold values from -0.03125 to 0.03125
- applied: float32 [2048, 28672], P(('row', 'col')), may hold values from -24 to 24
Outputs:
- hamiltonian: float32 [2048, 2048], P('col', 'row')
- intersection: float32 [2048, 2048], P('col', 'row')
All inputs are finite; a program needn't handle non-finite values.
Results may differ from a plain program's by a relative error of at most 0.000098.
Values sent between devices are 32-bit elements; how exact they have to be, the bound alone decides.
A program may use at most 64 MiB of HBM per device.

v0:
```python
import jax
import jax.numpy as jnp
from jax import lax
from jax.sharding import PartitionSpec as P


def sent_together(arrays, axis, dim, along):
    both = jnp.concatenate(arrays, axis=along)
    result, at, done = (lax.psum_scatter(both, axis, scatter_dimension=dim, tiled=True), 0, [])
    for a in arrays:
        done.append(lax.slice_in_dim(result, at, at + a.shape[along], axis=along))
        at += a.shape[along]
    return tuple(done)


def product(left, right):
    return lax.dot_general(
        left,
        right,
        (((1,), (1,)), ((), ())),
        precision=lax.Precision.HIGHEST,
        preferred_element_type=jnp.float32,
    )


def shards(orbitals, applied):
    mine_orb, mine_app = (
        lax.all_to_all(orbitals, "col", split_axis=1, concat_axis=0, tiled=True),
        lax.all_to_all(applied, "col", split_axis=1, concat_axis=0, tiled=True),
    )
    every_orb = lax.all_gather(mine_orb, "row", axis=0, tiled=True)
    ham_part = product(every_orb, mine_app)
    ovl_part = product(every_orb, mine_orb)
    hamiltonian, intersection = sent_together((ham_part, ovl_part), "col", 0, 1)
    return (hamiltonian, intersection)


def solution(mesh):
    placed = (P(("row", "col"), None), P(("row", "col"), None))
    return jax.shard_map(
        shards,
        mesh=mesh,
        in_specs=placed,
        out_specs=(P("col", "row"), P("col", "row")),
        check_vma=False,
    )
```

profile of v0, /device:TPU:8, one launch (start us, length us, event | category | flops | bytes accessed | tf_op | source)
XLA Modules:
  0.0 355.5 jit_solution(10867969578513426620)
XLA Ops:
  7.2 0.0 all-gather.2.cloned.1.call-start
  7.2 32.4 %all_to_all.38 = f32[8,16,1792]{2,0,1:T(8,128)} all-to-all(f32[8,16,1792]{2,0,1:T(8,128)} %bitcast.15), channel_id=1, replica_groups=mesh['row'=16,'col'=16] {'col'}, dimensions={1} | all-to-all | bytes 1835008 | tf_op jit(solution)/shard_map/all_to_all | solution.py:28
  39.6 0.0 all-gather.2.cloned.1.call-update
  39.7 3.6 %all-to-all-start.1 = ((f32[8,16,1792]{2,0,1:T(8,128)}), f32[8,16,1792]{2,0,1:T(8,128)S(1)}, u32[]{:S(2)}, u32[]{:S(2)}) async-start(f32[8,16,1792]{2,0,1:T(8,128)} %bitcast.16), calls=%async_computation.1 | async-start | bytes 1835008 | tf_op jit(solution)/shard_map/all_to_all | solution.py:29
  43.3 0.0 reduce-scatter.2.cloned.1.call-start
  43.4 173.2 %all-gather.2.cloned.1.call-done = f32[2048,1792]{1,0:T(8,128)} async-done(((f32[128,1792]{1,0:T(8,128)}), f32[2048,1792]{1,0:T(8,128)}) %all-gather.2.cloned.1.call-update) | async-done | bytes 14680080 | tf_op jit(solution)/shard_map/all_gather | solution.py:31
  216.6 18.5 %fusion.2 = f32[2048,128]{0,1:T(8,128)S(1)} fusion(f32[2048,1792]{1,0:T(8,128)} %all-gather.2.cloned.1.call-done, f32[8,16,1792]{2,0,1:T(8,128)} %all_to_all.38), kind=kOutput, calls=%fused_computation.3 | convolution fusion | flops 5637144576 | bytes 16646144 | tf_op jit(solution)/shard_map/dot_general | solution.py:17
  235.1 0.0 all-to-all-done.1
  235.2 18.3 %fusion = f32[2048,128]{0,1:T(8,128)S(1)} fusion(f32[2048,1792]{1,0:T(8,128)} %all-gather.2.cloned.1.call-done, f32[8,16,1792]{2,0,1:T(8,128)S(1)} %all-to-all-done.1), kind=kOutput, calls=%fused_computation.1 | convolution fusion | flops 5637144576 | bytes 16646144 | tf_op jit(solution)/shard_map/dot_general | solution.py:17
  253.5 1.5 pad_maximum_fusion
  255.0 0.0 reduce-scatter.2.cloned.1.call-update
  255.0 91.3 %reduce-scatter.2.cloned.1.call-done = f32[128,256]{0,1:T(8,128)} async-done(((f32[2048,256]{0,1:T(8,128)}), f32[128,256]{0,1:T(8,128)}) %reduce-scatter.2.cloned.1.call-update) | async-done | bytes 131088 | tf_op jit(solution)/shard_map/reduce_scatter | solution.py:9
  346.4 0.9 fusion.4
  347.2 0.7 copy.5
  348.0 0.7 copy.4
Async XLA Ops:
  7.2 209.5 %all-gather.2.cloned.1.call-start = ((), (), s32[]{:S(2)}) async-start(), calls=%async_computation.3 | async-start | bytes 15597568 | tf_op jit(solution)/shard_map/all_gather | solution.py:31
  39.7 195.5 %all-to-all-start.1 = ((f32[8,16,1792]{2,0,1:T(8,128)}), f32[8,16,1792]{2,0,1:T(8,128)S(1)}, u32[]{:S(2)}, u32[]{:S(2)}) async-start(f32[8,16,1792]{2,0,1:T(8,128)} %bitcast.16), calls=%async_computation.1 | async-start | bytes 1835008 | tf_op jit(solution)/shard_map/all_to_all | solution.py:29
  43.3 303.0 %reduce-scatter.2.cloned.1.call-start = ((), (), s32[]{:S(2)}) async-start(), calls=%async_computation.4 | async-start | bytes 2228224 | tf_op jit(solution)/shard_map/reduce_scatter | solution.py:9
Sparse Core Ops, SparseCore 0:
  39.8 176.7 all-gather.1
  255.1 91.1 reduce-scatter.1
where the time goes:
time: 356 us
  waiting for transfers between devices  265 us (74%)
  matrix products  36.8 us (10%)
  blocking collectives  32.4 us (9%)
  between operations  14.1 us (4%)
  starting transfers between devices  3.73 us (1%)
    all_gather x1, waiting for transfers between devices, shards(): every_orb = lax.all_gather(mine_orb, 'row', axis=0, tiled=True)  173 us
    reduce_scatter x1, waiting for transfers between devices, sent_together(): lax.psum_scatter(both, axis, scatter_dimension=dim, tiled=True)  91.3 us
    dot_general x2, matrix products, product(): lax.dot_general(left, right, (((1,), (1,)), ((), ())), precision=lax.Prec...  36.8 us
    all_to_all x1, blocking collectives, shards(): lax.all_to_all(orbitals, 'col', split_axis=1, concat_axis=0, tiled=True)  32.4 us
  transfers between devices with their start and end apart: 3, of which 2 were waited for; matrix products, arithmetic and copies ran while one was open for 5% of the time, Pallas kernels for 0%

commit v1 on v0

--- a/solution.py
+++ b/solution.py
@@ -28,7 +28,9 @@
         lax.all_to_all(orbitals, "col", split_axis=1, concat_axis=0, tiled=True),
         lax.all_to_all(applied, "col", split_axis=1, concat_axis=0, tiled=True),
     )
-    every_orb = lax.all_gather(mine_orb, "row", axis=0, tiled=True)
+    every_orb = jnp.concatenate(
+        lax.all_to_all(jnp.stack([mine_orb] * lax.axis_size("row")), "row", 0, 0), axis=0
+    )
     ham_part = product(every_orb, mine_app)
     ovl_part = product(every_orb, mine_orb)
     hamiltonian, intersection = sent_together((ham_part, ovl_part), "col", 0, 1)

time: 356 us -> 516 us (1.45)
  blocking collectives: 32.4 us -> 362 us
  waiting for transfers between devices: 265 us -> 93.5 us
    all_to_all x0 -> x1, blocking collectives: none -> 330 us  [shards(): lax.all_to_all(jnp.stack([mine_orb] * lax.axis_size('row')), 'row', 0, 0)]
    all_gather x1 -> x0, waiting for transfers between devices: 173 us -> none  [shards(): every_orb = lax.all_gather(mine_orb, 'row', axis=0, tiled=True)]
  transfers between devices with their start and end apart: 3 -> 2, of which waited for: 2 -> 2; matrix products, arithmetic and copies ran while one was open for 5% -> 4% of each run, Pallas kernels for 0% -> 0%
where the time goes in v1:
time: 516 us; the launch traced here: 515 us
  blocking collectives  362 us (70%)
  waiting for transfers between devices  93.5 us (18%)
  matrix products  36.7 us (7%)
  between operations  14.1 us (3%)
    all_to_all x1, blocking collectives, shards(): lax.all_to_all(jnp.stack([mine_orb] * lax.axis_size('row')), 'row', 0, 0)  330 us
    reduce_scatter x1, waiting for transfers between devices, sent_together(): lax.psum_scatter(both, axis, scatter_dimension=dim, tiled=True)  92.8 us
    dot_general x2, matrix products, product(): lax.dot_general(left, right, (((1,), (1,)), ((), ())), precision=lax.Prec...  36.7 us
    all_to_all x1, blocking collectives, shards(): lax.all_to_all(orbitals, 'col', split_axis=1, concat_axis=0, tiled=True)  32.3 us
  transfers between devices with their start and end apart: 2, of which 2 were waited for; matrix products, arithmetic and copies ran while one was open for 4% of the time, Pallas kernels for 0%

profile of v1, /device:TPU:8, one launch (start us, length us, event | category | flops | bytes accessed | tf_op | source)
XLA Modules:
  0.0 515.3 jit_solution(2663192728453900688)
XLA Ops:
  7.2 32.3 %all_to_all.40 = f32[8,16,1792]{2,0,1:T(8,128)S(1)} all-to-all(f32[8,16,1792]{2,0,1:T(8,128)} %bitcast.18), channel_id=1, replica_groups=mesh['row'=16,'col'=16] {'col'}, dimensions={1} | all-to-all | bytes 1835008 | tf_op jit(solution)/shard_map/all_to_all | solution.py:28
  39.5 1.4 stack.5
  40.9 329.9 %all_to_all.41 = f32[16,128,1792]{2,1,0:T(8,128)} all-to-all(f32[16,128,1792]{2,1,0:T(8,128)S(1)} %stack.5), channel_id=1, replica_groups=mesh['row'=16,'col'=16] {'row'}, dimensions={0} | all-to-all | bytes 29360128 | tf_op jit(solution)/shard_map/all_to_all | solution.py:32
  370.8 3.6 all-to-all-start.2
  374.4 0.0 reduce-scatter.2.cloned.1.call-start
  374.5 18.3 %fusion.2 = f32[2048,128]{0,1:T(8,128)S(1)} fusion(f32[2048,1792]{1,0:T(8,128)} %bitcast.15, f32[8,16,1792]{2,0,1:T(8,128)S(1)} %all_to_all.40), kind=kOutput, calls=%fused_computation.3 | convolution fusion | flops 5637144576 | bytes 16646144 | tf_op jit(solution)/shard_map/dot_general | solution.py:17
  392.8 0.7 all-to-all-done.2
  393.5 18.3 %fusion = f32[2048,128]{0,1:T(8,128)S(1)} fusion(f32[2048,1792]{1,0:T(8,128)} %bitcast.16, f32[8,16,1792]{2,0,1:T(8,128)S(1)} %all-to-all-done.2), kind=kOutput, calls=%fused_computation.1 | convolution fusion | flops 5637144576 | bytes 16646144 | tf_op jit(solution)/shard_map/dot_general | solution.py:17
  411.9 1.5 pad_maximum_fusion
  413.3 0.0 reduce-scatter.2.cloned.1.call-update
  413.4 92.8 %reduce-scatter.2.cloned.1.call-done = f32[128,256]{0,1:T(8,128)} async-done(((f32[2048,256]{0,1:T(8,128)}), f32[128,256]{0,1:T(8,128)}) %reduce-scatter.2.cloned.1.call-update) | async-done | bytes 131088 | tf_op jit(solution)/shard_map/reduce_scatter | solution.py:9
  506.1 0.9 fusion.4
  507.0 0.7 copy.4
  507.8 0.7 copy.5
Async XLA Ops:
  370.8 22.7 %all-to-all-start.2 = ((f32[8,16,1792]{2,0,1:T(8,128)}), f32[8,16,1792]{2,0,1:T(8,128)S(1)}, u32[]{:S(2)}, u32[]{:S(2)}) async-start(f32[8,16,1792]{2,0,1:T(8,128)} %bitcast.4), calls=%async_computation.2 | async-start | bytes 1835008 | tf_op jit(solution)/shard_map/all_to_all | solution.py:29
  374.4 131.7 %reduce-scatter.2.cloned.1.call-start = ((), (), s32[]{:S(2)}) async-start(), calls=%async_computation.4 | async-start | bytes 2228224 | tf_op jit(solution)/shard_map/reduce_scatter | solution.py:9
Sparse Core Ops, SparseCore 0:
  413.5 92.6 reduce-scatter.1
